TPU v7x, 8 devices: a whole 2x2x1 slice. The times are simulated.
8 devices in a mesh: dp: 1 (over z), sp: 2 (over y), tp: 4 (over x, core).
Axes of the slice: x: 2, y: 2, z: 1, core: 2. Of those that a mesh axis runs over, the one named last changes fastest.
Arguments:
- latents: bfloat16 [1, 256, 1280], P('dp')
- queries: bfloat16 [1, 512, 768], P('dp', 'sp')
- lat_ln1: float32 [1280], replicated
- lat_wq: bfloat16 [1280, 8, 160], P(None, 'tp')
- lat_wk: bfloat16 [1280, 8, 160], P(None, 'tp')
- lat_wv: bfloat16 [1280, 8, 160], P(None, 'tp')
- lat_wo: bfloat16 [8, 160, 1280], P('tp')
- lat_ln2: float32 [1280], replicated
- lat_up: bfloat16 [1280, 1280], P(None, 'tp')
- lat_down: bfloat16 [1280, 1280], P('tp')
- dec_lnq: float32 [768], replicated
- dec_lnkv: float32 [1280], replicated
- dec_wq: bfloat16 [768, 768], replicated
- dec_wk: bfloat16 [1280, 768], replicated
- dec_wv: bfloat16 [1280, 768], replicated
- dec_wo: bfloat16 [768, 768], replicated
- dec_ln: float32 [768], replicated
- dec_up: bfloat16 [768, 768], replicated
- dec_down: bfloat16 [768, 768], replicated
- dec_out: bfloat16 [768, 32000], replicated
Outputs:
- output: bfloat16 [1, 512, 32000], P('dp', 'sp')
All inputs are finite; a program needn't handle non-finite values.
Results may differ from a plain program's by a relative error of at most 0.0194839.
Values are sent between devices in bfloat16 or wider.
A program may use at most 1 GiB of HBM per device.

v0:
```python
import jax
import jax.numpy as jnp
from jax import lax
from jax.sharding import PartitionSpec as P

LN_EPS = 1e-5


def layer_norm(rows_in, gain_vec):
    widened = rows_in.astype(jnp.float32)
    row_mean = jnp.mean(widened, axis=-1, keepdims=True)
    row_var = jnp.mean(jnp.square(widened - row_mean), axis=-1, keepdims=True)
    return ((widened - row_mean) * lax.rsqrt(row_var + LN_EPS) * gain_vec).astype(jnp.bfloat16)


def decode_rows(query_rows, all_keys, all_values, dec_lnq, dec_wq, dec_wo, dec_ln, dec_up, dec_down, dec_out):
    q_proj = jnp.dot(layer_norm(query_rows, dec_lnq), dec_wq, preferred_element_type=jnp.float32).astype(jnp.bfloat16)
    scores = jnp.einsum("crd,cld->crl", q_proj, all_keys, preferred_element_type=jnp.float32) * dec_wq.shape[1] ** -0.5
    attn_probs = jax.nn.softmax(scores, axis=-1).astype(jnp.bfloat16)
    context = jnp.einsum("crl,cld->crd", attn_probs, all_values, preferred_element_type=jnp.float32).astype(jnp.bfloat16)
    mixed_rows = (q_proj.astype(jnp.float32) + jnp.dot(context, dec_wo, preferred_element_type=jnp.float32)).astype(jnp.bfloat16)
    hidden = jax.nn.gelu(jnp.dot(layer_norm(mixed_rows, dec_ln), dec_up, preferred_element_type=jnp.float32), approximate=False).astype(jnp.bfloat16)
    final_rows = (mixed_rows.astype(jnp.float32) + jnp.dot(hidden, dec_down, preferred_element_type=jnp.float32)).astype(jnp.bfloat16)
    return jnp.dot(final_rows, dec_out, preferred_element_type=jnp.float32).astype(jnp.bfloat16)


def solution(mesh):
    tp_size = mesh.shape["tp"]
    head_split = P(None, "tp", None)
    whole_vec = P(None)
    whole_mat = P(None, None)
    in_specs = (P("dp", None, None), P("dp", "sp", None), whole_vec, head_split, head_split, head_split, P("tp", None, None), whole_vec, P(None, "tp"), P("tp", None), whole_vec, whole_vec, whole_mat, whole_mat, whole_mat, whole_mat, whole_vec, whole_mat, whole_mat, whole_mat)

    def local_step(latents, queries, lat_ln1, lat_wq, lat_wk, lat_wv, lat_wo, lat_ln2, lat_up, lat_down, dec_lnq, dec_lnkv, dec_wq, dec_wk, dec_wv, dec_wo, dec_ln, dec_up, dec_down, dec_out):
        tp_index = lax.axis_index("tp")
        head_dim = lat_wq.shape[2]
        normed = layer_norm(latents, lat_ln1)
        q_heads = jnp.einsum("bnd,dhe->bnhe", normed, lat_wq, preferred_element_type=jnp.float32).astype(jnp.bfloat16)
        k_heads = jnp.einsum("bnd,dhe->bnhe", normed, lat_wk, preferred_element_type=jnp.float32).astype(jnp.bfloat16)
        v_heads = jnp.einsum("bnd,dhe->bnhe", normed, lat_wv, preferred_element_type=jnp.float32).astype(jnp.bfloat16)
        scores = jnp.einsum("bqhe,bkhe->bhqk", q_heads, k_heads, preferred_element_type=jnp.float32) * head_dim ** -0.5
        attn_probs = jax.nn.softmax(scores, axis=-1).astype(jnp.bfloat16)
        context = jnp.einsum("bhqk,bkhe->bqhe", attn_probs, v_heads, preferred_element_type=jnp.float32).astype(jnp.bfloat16)
        attn_part = jnp.einsum("crif,ife->cre", context, lat_wo, preferred_element_type=jnp.float32).astype(jnp.bfloat16)
        attn_sum = lax.psum(attn_part, "tp")
        z_mid = (latents.astype(jnp.float32) + attn_sum.astype(jnp.float32)).astype(jnp.bfloat16)
        hidden = jax.nn.gelu(jnp.dot(layer_norm(z_mid, lat_ln2), lat_up, preferred_element_type=jnp.float32), approximate=False).astype(jnp.bfloat16)
        mlp_part = jnp.dot(hidden, lat_down, preferred_element_type=jnp.float32).astype(jnp.bfloat16)
        mlp_rows = lax.psum_scatter(mlp_part, "tp", scatter_dimension=1, tiled=True)
        row_count = mlp_rows.shape[1]
        mid_rows = lax.dynamic_slice_in_dim(z_mid, tp_index * row_count, row_count, axis=1)
        new_rows = (mid_rows.astype(jnp.float32) + mlp_rows.astype(jnp.float32)).astype(jnp.bfloat16)
        kv_in = layer_norm(new_rows, dec_lnkv)
        key_rows = jnp.dot(kv_in, dec_wk, preferred_element_type=jnp.float32).astype(jnp.bfloat16)
        value_rows = jnp.dot(kv_in, dec_wv, preferred_element_type=jnp.float32).astype(jnp.bfloat16)
        all_keys = lax.all_gather(key_rows, "tp", axis=1, tiled=True)
        all_values = lax.all_gather(value_rows, "tp", axis=1, tiled=True)
        query_count = queries.shape[1] // tp_size
        query_rows = lax.dynamic_slice_in_dim(queries, tp_index * query_count, query_count, axis=1)
        out_rows = decode_rows(query_rows, all_keys, all_values, dec_lnq, dec_wq, dec_wo, dec_ln, dec_up, dec_down, dec_out)
        return lax.all_gather(out_rows, "tp", axis=1, tiled=True)

    return jax.shard_map(local_step, mesh=mesh, in_specs=in_specs, out_specs=P("dp", "sp", None), check_vma=False)
```

profile of v0, /device:TPU:0, one launch (start us, length us, event | category | flops | bytes accessed | tf_op | source)
XLA Modules:
  0.0 236.6 jit_solution(18429251229871192585)
XLA Ops:
  6.6 1.4 convert_reduce_fusion
  8.0 1.4 fusion.8
  9.7 0.4 fusion.277
  10.2 0.4 copy-done.7
  10.6 0.4 fusion.276
  11.4 0.4 fusion.275
  12.2 2.8 %fusion.3 = bf16[1,256,1280]{2,1,0:T(8,128)(2,1)} fusion(bf16[2,160,1280]{2,1,0:T(8,128)(2,1)} %param.26, f32[2,256]{1,0:T(2,128)S(1)} %fusion.272, f32[256,2,160]{0,2,1:T(8,128)S(1)} %bitcast.68, f32[2,256,256]{1,2,0:T(8,128)S(1)} %convolution_multiply_fusion), kind=kOutput, calls=%fused_computation.6 | convolution fusion | flops 252543744 | bytes 2328576 | tf_op jit(solution)/shard_map/crif,ife->cre/dot_general | solution.py:44
  15.0 31.2 %all-reduce.2.cloned.1.call-done = bf16[1,256,1280]{2,1,0:T(8,128)(2,1)} async-done(((bf16[1,256,1280]{2,1,0:T(8,128)(2,1)}), bf16[1,256,1280]{2,1,0:T(8,128)(2,1)}) %all-reduce.2.cloned.1.call-update) | async-done | bytes 655376 | tf_op jit(solution)/shard_map/psum | solution.py:45
  46.2 1.4 convert_reduce_fusion.1
  47.9 4.3 %fusion.2 = bf16[1,256,1280]{2,1,0:T(8,128)(2,1)} fusion(bf16[320,1280]{1,0:T(8,128)(2,1)} %param.29, bf16[1280,320]{0,1:T(8,128)(2,1)} %param.28, bf16[1,256,1280]{2,1,0:T(8,128)(2,1)S(1)} %get-tuple-element.8, f32[1280]{0:T(1024)S(1)} %copy-done.15, f32[256]{0:T(256)S(1)} %add_rsqrt_fusion, f32[256]{0:T(256)S(1)} %broadcast_multiply_fusion), kind=kOutput, calls=%fused_computation.5 | convolution fusion | flops 426721280 | bytes 2956288 | tf_op jit(solution)/shard_map/dot_general | solution.py:48
  52.7 1.6 convolution_convert_fusion.3
  54.4 15.0 %reduce-scatter.2.cloned.1.call-done = bf16[1,64,1280]{2,1,0:T(8,128)(2,1)} async-done(((bf16[1,256,1280]{2,1,0:T(8,128)(2,1)}), bf16[1,64,1280]{2,1,0:T(8,128)(2,1)}) %reduce-scatter.2.cloned.1.call-update) | async-done | bytes 163856 | tf_op jit(solution)/shard_map/reduce_scatter | solution.py:49
  69.3 1.1 convert_reduce_fusion.2
  70.7 0.5 convolution_convert_fusion.5
  71.2 0.8 copy-done.3
  72.0 0.5 convolution_convert_fusion.6
  72.5 8.5 %all-gather = bf16[256,768]{1,0:T(8,128)(2,1)S(1)} all-gather(bf16[64,768]{1,0:T(8,128)(2,1)S(1)} %convolution_convert_fusion.6), channel_id=2, replica_groups=mesh['dp'=1,'sp'=2,'tp'=4] {'tp'}, dimensions={0}, use_global_device_ids=true | all-gather | bytes 491520 | tf_op jit(solution)/shard_map/all_gather | solution.py:56
  81.0 9.7 %all-gather.1 = bf16[256,768]{1,0:T(8,128)(2,1)S(1)} all-gather(bf16[64,768]{1,0:T(8,128)(2,1)S(1)} %convolution_convert_fusion.5), channel_id=3, replica_groups=mesh['dp'=1,'sp'=2,'tp'=4] {'tp'}, dimensions={0}, use_global_device_ids=true | all-gather | bytes 491520 | tf_op jit(solution)/shard_map/all_gather | solution.py:57
  91.2 0.6 fusion.274
  92.1 0.4 fusion.101
  92.5 0.7 copy-done.14
  93.2 21.1 %convolution_convert_fusion = bf16[64,32000]{1,0:T(8,128)(2,1)} fusion(bf16[768,32000]{1,0:T(8,128)(2,1)} %param.39, f32[64,768]{1,0:T(8,128)S(1)} %get-tuple-element.12, bf16[768,768]{1,0:T(8,128)(2,1)S(1)} %copy-done.14, f32[64,768]{1,0:T(8,128)S(1)} %fusion.101), kind=kOutput, calls=%fused_computation.1 | convolution fusion | flops 3226566656 | bytes 54820864 | tf_op jit(solution)/shard_map/dot_general | solution.py:24
  114.3 102.1 %all-gather.5.cloned.1.call-done = bf16[256,32000]{1,0:T(8,128)(2,1)} async-done(((bf16[64,32000]{1,0:T(8,128)(2,1)}), bf16[256,32000]{1,0:T(8,128)(2,1)}) %all-gather.5.cloned.1.call-update) | async-done | bytes 16384016 | tf_op jit(solution)/shard_map/all_gather | solution.py:61
  216.4 13.7 %copy.25 = bf16[1,256,32000]{2,1,0:T(8,128)(2,1)} copy(bf16[1,256,32000]{2,1,0:T(8,128)(2,1)} %bitcast.62) | data formatting | bytes 32768000
  (55 shorter events, 3.0 us)
Async XLA Ops:
  6.5 64.1 %copy-start = (bf16[1280,768]{1,0:T(8,128)(2,1)S(1)}, bf16[1280,768]{1,0:T(8,128)(2,1)}, u32[]{:S(2)}) copy-start(bf16[1280,768]{1,0:T(8,128)(2,1)} %param.34) | copy-start | bytes 5898244
  6.5 2.9 %copy-start.2 = (bf16[1,256,1280]{2,1,0:T(8,128)(2,1)S(1)}, bf16[1,256,1280]{2,1,0:T(8,128)(2,1)}, u32[]{:S(2)}) copy-start(bf16[1,256,1280]{2,1,0:T(8,128)(2,1)} %param.20) | copy-start | bytes 1966084
  6.5 2.9 %copy-start.11 = (f32[1280]{0:T(1024)S(1)}, f32[1280]{0:T(1024)}, u32[]{:S(2)}) copy-start(f32[1280]{0:T(1024)} %param.22) | copy-start | bytes 15364
  6.5 3.2 %copy-start.6 = (bf16[1280,2,160]{0,2,1:T(8,128)(2,1)S(1)}, bf16[1280,2,160]{0,2,1:T(8,128)(2,1)}, u32[]{:S(2)}) copy-start(bf16[1280,2,160]{0,2,1:T(8,128)(2,1)} %param.24) | copy-start | bytes 2457604
  6.5 39.7 %all-reduce.2.cloned.1.call-start = ((), (), s32[]{:S(2)}) async-start(), calls=%async_computation.1 | async-start | bytes 1310720 | tf_op jit(solution)/shard_map/psum | solution.py:45
  9.4 1.1 copy-start.7
  10.2 1.2 copy-start.8
  15.0 32.9 %copy-start.15 = (f32[1280]{0:T(1024)S(1)}, f32[1280]{0:T(1024)}, u32[]{:S(2)}) copy-start(f32[1280]{0:T(1024)} %param.27) | copy-start | bytes 15364
  15.0 54.3 %reduce-scatter.2.cloned.1.call-start = ((), (), s32[]{:S(2)}) async-start(), calls=%async_computation.2 | async-start | bytes 819200 | tf_op jit(solution)/shard_map/reduce_scatter | solution.py:49
  47.9 4.4 %copy-start.9 = (bf16[1,256,768]{2,1,0:T(8,128)(2,1)S(1)}, bf16[1,256,768]{2,1,0:T(8,128)(2,1)}, u32[]{:S(2)}) copy-start(bf16[1,256,768]{2,1,0:T(8,128)(2,1)} %param.21) | copy-start | bytes 1179652
  47.9 4.8 %copy-start.12 = (f32[768]{0:T(1024)S(1)}, f32[768]{0:T(1024)}, u32[]{:S(2)}) copy-start(f32[768]{0:T(1024)} %param.30) | copy-start | bytes 9220
  52.3 18.4 %copy-start.10 = (f32[1280]{0:T(1024)S(1)}, f32[1280]{0:T(1024)}, u32[]{:S(2)}) copy-start(f32[1280]{0:T(1024)} %param.31) | copy-start | bytes 15364
  52.3 164.1 %all-gather.5.cloned.1.call-start = ((), (), s32[]{:S(2)}) async-start(), calls=%async_computation.3 | async-start | bytes 20480000 | tf_op jit(solution)/shard_map/all_gather | solution.py:61
  70.4 1.6 copy-start.3
  72.5 18.7 %copy-start.5 = (bf16[768,768]{1,0:T(8,128)(2,1)S(1)}, bf16[768,768]{1,0:T(8,128)(2,1)}, u32[]{:S(2)}) copy-start(bf16[768,768]{1,0:T(8,128)(2,1)} %param.35) | copy-start | bytes 3538948
  90.6 1.4 copy-start.4
  90.6 1.4 copy-start.13
  91.9 1.3 copy-start.14
  216.4 13.7 %copy-start.1 = (bf16[1280,768]{1,0:T(8,128)(2,1)S(1)}, bf16[1280,768]{1,0:T(8,128)(2,1)}, u32[]{:S(2)}) copy-start(bf16[1280,768]{1,0:T(8,128)(2,1)} %param.34) | copy-start | bytes 5898244
Sparse Core Ops, SparseCore 0:
  15.1 31.0 all-reduce.1
  52.4 16.8 reduce-scatter.1
  114.4 101.9 all-gather.4
where the time goes:
time: 237 us
  waiting for transfers between devices  148 us (62%)
  matrix products  33.7 us (14%)
  blocking collectives  18.1 us (8%)
  local copies, waits for them, and re-layouts  16 us (7%)
  between operations  13.4 us (6%)
  other arithmetic  6.93 us (3%)
    all_gather x1, waiting for transfers between devices, local_step(): return lax.all_gather(out_rows, 'tp', axis=1, tiled=True)  102 us
    psum x1, waiting for transfers between devices, local_step(): attn_sum = lax.psum(attn_part, 'tp')  31.2 us
    dot_general x1, matrix products, decode_rows(): jnp.dot(final_rows, dec_out, preferred_element_type=jnp.float32)  21.1 us
    unnamed x33, local copies, waits for them, and re-layouts  16 us
    reduce_scatter x1, waiting for transfers between devices, local_step(): mlp_rows = lax.psum_scatter(mlp_part, 'tp', scatter_dimension=1, tiled=True)  15 us
    all_gather x1, blocking collectives, local_step(): all_values = lax.all_gather(value_rows, 'tp', axis=1, tiled=True)  9.65 us
    all_gather x1, blocking collectives, local_step(): all_keys = lax.all_gather(key_rows, 'tp', axis=1, tiled=True)  8.5 us
  transfers between devices with their start and end apart: 3, of which 3 were waited for; matrix products, arithmetic and copies ran while one was open for 1% of the time, Pallas kernels for 0%

commit v1 on v0

v1 whole, which is shorter than its diff:
```python
import functools

import jax
import jax.numpy as jnp
from jax import lax
from jax.experimental import pallas as pl
from jax.experimental.pallas import tpu as pltpu
from jax.sharding import PartitionSpec as P

LN_EPS = 1e-5
MESH = pl.DeviceIdType.MESH
BF16 = jnp.bfloat16
F32 = jnp.float32

CHUNKS = 2
PRE_COLS = 28160
BLOCK = 6400


def dot(a, b):
    return lax.dot_general(a, b, (((1,), (0,)), ((), ())), preferred_element_type=F32)


def dot_nt(a, b):
    return lax.dot_general(a, b, (((1,), (1,)), ((), ())), preferred_element_type=F32)


def norm_rows(wide, gain):
    mean = jnp.mean(wide, axis=-1, keepdims=True)
    cent = wide - mean
    var = jnp.mean(cent * cent, axis=-1, keepdims=True)
    return (cent * lax.rsqrt(var + LN_EPS) * gain).astype(BF16)


def gelu(v):
    return 0.5 * v * (1.0 + lax.erf(v * (0.5**0.5)))


def softmax_rows(scores, scale):
    scaled = scores * scale
    top = jnp.max(scaled, axis=-1, keepdims=True)
    expd = jnp.exp(scaled - top)
    return (expd * (1.0 / jnp.sum(expd, axis=-1, keepdims=True))).astype(BF16)


def front_kernel(
    lat_in, qry_in, g1_in, wq_in, wk_in, wv_in, wo_in, g2_in, up_in, down_in,
    gq_in, gkv_in, dwq_in, dwk_in, dwv_in, dwo_in, gd_in, dup_in, ddown_in, out_in,
    pre_out, x2_out,
    z, normed, qry, g1, g2, gq, gkv, gd, wq, wk, wv, wo, up, down, dwq, dwk, dwv, dwo, dup, ddown,
    q_h, k_h, v_h, ctx_mine, ctx_send, ctx_recv,
    part1, recv1, mid, part2, recv2, kv_in, qd, kd, vd, mixed,
    load_sem, pre_sem, send_sem, recv_sem,
):
    s = lax.axis_index("sp")
    t = lax.axis_index("tp")
    c = lax.rem(t, 2)
    partner = {"tp": t + 1 - 2 * c}
    across_x = {"tp": lax.rem(t + 2, 4)}
    across_y = {"sp": 1 - s}

    heads, head_dim = wq.shape[0], wq.shape[1]
    rows = z.shape[0]
    half = rows // 2
    mine = half // 2
    step = mine // CHUNKS
    mlp = down_in.shape[0]

    barrier = pltpu.get_barrier_semaphore()
    for peer in (partner, across_x, across_y):
        pl.semaphore_signal(barrier, inc=1, device_id=peer, device_id_type=MESH)

    loads = {}

    def load(name, src, dst):
        copy = pltpu.make_async_copy(src, dst, load_sem.at[len(loads)])
        copy.start()
        loads[name] = copy

    load("z", lat_in, z)
    load("g1", g1_in, g1)
    load("wk", wk_in, wk)
    load("wq", wq_in, wq)
    load("wv", wv_in, wv)
    load("wo", wo_in, wo.at[pl.ds(0, heads * head_dim)])
    load("qry", qry_in, qry)
    load("gq", gq_in, gq)
    load("g2", g2_in, g2)
    load("gkv", gkv_in, gkv)
    load("gd", gd_in, gd)
    load("up", up_in, up.at[pl.ds(0, mlp)])
    load("down", down_in, down.at[pl.ds(0, mlp)])
    load("dwq", dwq_in, dwq)
    load("dwk", dwk_in, dwk)
    load("dwv", dwv_in, dwv)
    load("dwo", dwo_in, dwo)
    load("dup", dup_in, dup)
    load("ddown", ddown_in, ddown)

    pre_pieces = pre_sem.shape[0]
    pre_rows = pre_out.shape[0] // pre_pieces
    pre = []
    for i in range(pre_pieces):
        band = pl.ds(i * pre_rows, pre_rows)
        copy = pltpu.make_async_copy(out_in.at[band, pl.ds(0, PRE_COLS)], pre_out.at[band], pre_sem.at[i])
        copy.start(priority=1)
        pre.append(copy)

    def send(i, src, dst, peer):
        copy = pltpu.make_async_remote_copy(
            src_ref=src, dst_ref=dst, send_sem=send_sem.at[i], recv_sem=recv_sem.at[i], device_id=peer, device_id_type=MESH
        )
        copy.start()
        return copy

    pl.semaphore_wait(barrier, 3)
    swap_wo = send(0, wo_in, wo.at[pl.ds(heads * head_dim, heads * head_dim)], partner)
    swap_up = send(1, up_in, up.at[pl.ds(mlp, mlp)], partner)
    swap_down = send(2, down_in, down.at[pl.ds(mlp, mlp)], partner)

    loads["z"].wait()
    loads["g1"].wait()
    gain1 = g1[...]
    for r in range(0, rows, 16):
        normed[pl.ds(r, 16), :] = norm_rows(z[pl.ds(r, 16), :].astype(F32), gain1)
    loads["wk"].wait()
    for h in range(heads):
        k_h[h] = dot_nt(normed[...], wk[h]).astype(BF16)
    loads["wq"].wait()
    own_half = normed[pl.ds(pl.multiple_of(s * half, half), half), :]
    for h in range(heads):
        q_h[h] = dot_nt(own_half, wq[h]).astype(BF16)
    loads["wv"].wait()
    for h in range(heads):
        v_h[h] = dot_nt(normed[...], wv[h]).astype(BF16)

    def attend(first, dst):
        for h in range(heads):
            scores = dot_nt(q_h[h, pl.ds(first, mine), :], k_h[h])
            probs = softmax_rows(scores, head_dim**-0.5)
            dst[h, :, pl.ds(0, head_dim)] = dot(probs, v_h[h]).astype(BF16)

    attend(pl.multiple_of((1 - c) * mine, mine), ctx_send)
    swap_ctx = send(3, ctx_send, ctx_recv, partner)
    attend(pl.multiple_of(c * mine, mine), ctx_mine)

    loads["wo"].wait()
    swap_wo.wait()
    swap_ctx.wait()
    first_sends, second_sends, kv_part, kv_y, kv_fwd = [], [], [], [], []
    base = 4
    for k in range(CHUNKS):
        band = pl.ds(k * step, step)
        total = None
        for src, row0 in ((ctx_mine, 0), (ctx_recv, heads * head_dim)):
            for h in range(heads):
                term = dot(src[h, band, pl.ds(0, head_dim)], wo[pl.ds(row0 + h * head_dim, head_dim), :])
                total = term if total is None else total + term
        part1[band, :] = total.astype(BF16)
        first_sends.append(send(base + k, part1.at[band], recv1.at[band], across_x))

    loads["qry"].wait()
    loads["gq"].wait()
    loads["dwq"].wait()
    gain_q = gq[...]
    query_rows = qry.shape[0]
    for r in range(0, query_rows, 16):
        mixed[pl.ds(r, 16), :] = norm_rows(qry[pl.ds(r, 16), :].astype(F32), gain_q)
    qd[...] = dot(mixed[...], dwq[...]).astype(BF16)

    for name in ("g2", "up", "down", "gkv"):
        loads[name].wait()
    swap_up.wait()
    swap_down.wait()
    gain2 = g2[...]
    gain_kv = gkv[...]
    base = 4 + CHUNKS
    row_first = s * half + c * mine
    for k in range(CHUNKS):
        band = pl.ds(k * step, step)
        first_sends[k].wait()
        zrows = z[pl.ds(pl.multiple_of(row_first + k * step, step), step), :].astype(F32)
        mid[band, :] = (zrows + (part1[band, :].astype(F32) + recv1[band, :].astype(F32))).astype(BF16)
        hidden = gelu(dot_nt(norm_rows(mid[band, :].astype(F32), gain2), up[...])).astype(BF16)
        part2[band, :] = dot(hidden, down[...]).astype(BF16)
        second_sends.append(send(base + k, part2.at[band], recv2.at[band], across_x))

    base = 4 + 2 * CHUNKS
    for k in range(CHUNKS):
        band = pl.ds(k * step, step)
        second_sends[k].wait()
        full = mid[band, :].astype(F32) + (part2[band, :].astype(F32) + recv2[band, :].astype(F32))
        kv_in[0, band, :] = norm_rows(full.astype(BF16).astype(F32), gain_kv)
        kv_y.append(send(base + k, kv_in.at[0, band], kv_in.at[2, band], across_y))
        kv_part.append(send(base + CHUNKS + k, kv_in.at[0, band], kv_in.at[1, band], partner))

    loads["dwk"].wait()
    loads["dwv"].wait()
    for k in range(CHUNKS):
        kv_part[k].wait()

    def keys_values(group):
        group_rows = jnp.concatenate([kv_in[2 * group], kv_in[2 * group + 1]], axis=0)
        band = pl.ds(group * half, half)
        kd[band, :] = dot(group_rows, dwk[...]).astype(BF16)
        vd[band, :] = dot(group_rows, dwv[...]).astype(BF16)

    keys_values(0)
    base = 4 + 4 * CHUNKS
    for k in range(CHUNKS):
        band = pl.ds(k * step, step)
        kv_y[k].wait()
        kv_fwd.append(send(base + k, kv_in.at[2, band], kv_in.at[3, band], partner))
    for k in range(CHUNKS):
        kv_fwd[k].wait()
    keys_values(1)

    for name in ("dwo", "gd", "dup", "ddown"):
        loads[name].wait()
    gain_d = gd[...]
    blk = query_rows // 2
    for q in range(2):
        band = pl.ds(q * blk, blk)
        probs = softmax_rows(dot_nt(qd[band, :], kd[...]), qd.shape[1] ** -0.5)
        context = dot(probs, vd[...]).astype(BF16)
        mixed[band, :] = (qd[band, :].astype(F32) + dot(context, dwo[...])).astype(BF16)
    for q in range(2):
        band = pl.ds(q * blk, blk)
        hidden = gelu(dot(norm_rows(mixed[band, :].astype(F32), gain_d), dup[...])).astype(BF16)
        x2_out[band, :] = (mixed[band, :].astype(F32) + dot(hidden, ddown[...])).astype(BF16)

    for copy in pre:
        copy.wait()


def out_kernel(x_ref, pre_ref, rest_hbm, o_ref, rest, stage, rest_sem, out_sem):
    total = o_ref.shape[1]
    pre_cols = pre_ref.shape[1]
    fetch = pltpu.make_async_copy(rest_hbm.at[:, pl.ds(pre_cols, total - pre_cols)], rest, rest_sem)
    fetch.start()
    copies = []
    first = 0
    widths = []
    left = pre_cols
    while left:
        widths.append((min(BLOCK, left), False))
        left -= widths[-1][0]
    left = total - pre_cols
    while left:
        widths.append((min(2560, left), True))
        left -= widths[-1][0]
    for i, (width, from_rest) in enumerate(widths):
        slot = i % 2
        if i >= 2:
            copies[i - 2].wait()
        if from_rest and not widths[i - 1][1]:
            fetch.wait()
        src, off = (rest, first - pre_cols) if from_rest else (pre_ref, first)
        stage[slot, :, pl.ds(0, width)] = dot(x_ref[...], src[:, pl.ds(off, width)]).astype(BF16)
        copy = pltpu.make_async_copy(stage.at[slot, :, pl.ds(0, width)], o_ref.at[:, pl.ds(first, width)], out_sem.at[slot])
        copy.start()
        copies.append(copy)
        first += width
    copies[-2].wait()
    copies[-1].wait()


def solution(mesh):
    head_split = P(None, "tp", None)
    whole_vec = P(None)
    whole_mat = P(None, None)
    in_specs = (P("dp", None, None), P("dp", "sp", None), whole_vec, head_split, head_split, head_split, P("tp", None, None), whole_vec, P(None, "tp"), P("tp", None), whole_vec, whole_vec, whole_mat, whole_mat, whole_mat, whole_mat, whole_vec, whole_mat, whole_mat, whole_mat)

    def local_step(latents, queries, lat_ln1, lat_wq, lat_wk, lat_wv, lat_wo, lat_ln2, lat_up, lat_down, dec_lnq, dec_lnkv, dec_wq, dec_wk, dec_wv, dec_wo, dec_ln, dec_up, dec_down, dec_out):
        rows, width = latents.shape[1:]
        query_rows, query_ch = queries.shape[1:]
        heads, head_dim = lat_wq.shape[1:]
        mlp = lat_up.shape[1]
        dec = dec_wq.shape[1]
        total = dec_out.shape[1]
        half, mine = rows // 2, rows // 4

        def flip(w):
            return jnp.transpose(w, (1, 2, 0))

        args = [
            latents[0], queries[0], lat_ln1[None], flip(lat_wq), flip(lat_wk), flip(lat_wv), lat_wo.reshape(heads * head_dim, width),
            lat_ln2[None], lat_up.T, lat_down, dec_lnq[None], dec_lnkv[None], dec_wq, dec_wk, dec_wv, dec_wo, dec_ln[None], dec_up, dec_down, dec_out,
        ]
        args = [pltpu.with_memory_space_constraint(a, pltpu.HBM) for a in args]

        def vm(*shape, dtype=BF16):
            return pltpu.VMEM(shape, dtype)

        scratch = [
            vm(rows, width), vm(rows, width), vm(query_rows, query_ch),
            vm(1, width, dtype=F32), vm(1, width, dtype=F32), vm(1, query_ch, dtype=F32), vm(1, width, dtype=F32), vm(1, dec, dtype=F32),
            vm(heads, head_dim, width), vm(heads, head_dim, width), vm(heads, head_dim, width),
            vm(2 * heads * head_dim, width), vm(2 * mlp, width), vm(2 * mlp, width),
            vm(query_ch, dec), vm(width, dec), vm(width, dec), vm(dec, dec), vm(dec, dec), vm(dec, dec),
            vm(heads, half, head_dim), vm(heads, rows, head_dim), vm(heads, rows, head_dim),
            vm(heads, mine, 256), vm(heads, mine, 256), vm(heads, mine, 256),
            vm(mine, width), vm(mine, width), vm(mine, width), vm(mine, width), vm(mine, width),
            vm(4, mine, width), vm(query_rows, dec), vm(rows, dec), vm(rows, dec), vm(query_rows, dec),
            pltpu.SemaphoreType.DMA((19,)), pltpu.SemaphoreType.DMA((8,)),
            pltpu.SemaphoreType.DMA((4 + 5 * CHUNKS,)), pltpu.SemaphoreType.DMA((4 + 5 * CHUNKS,)),
        ]
        pre, x2 = pl.pallas_call(
            front_kernel,
            out_shape=(pltpu.VMEM((dec, PRE_COLS), BF16), jax.ShapeDtypeStruct((query_rows, dec), BF16)),
            in_specs=[pl.BlockSpec(memory_space=pltpu.HBM)] * len(args),
            out_specs=(pl.BlockSpec(memory_space=pltpu.VMEM), pl.BlockSpec(memory_space=pltpu.VMEM)),
            scratch_shapes=scratch,
            compiler_params=pltpu.CompilerParams(collective_id=0, has_side_effects=True, vmem_limit_bytes=22 << 20),
            name="front",
        )(*args)
        out = pl.pallas_call(
            out_kernel,
            out_shape=jax.ShapeDtypeStruct((query_rows, total), BF16),
            in_specs=[pl.BlockSpec(memory_space=pltpu.VMEM), pl.BlockSpec(memory_space=pltpu.VMEM), pl.BlockSpec(memory_space=pltpu.HBM)],
            out_specs=pl.BlockSpec(memory_space=pltpu.HBM),
            scratch_shapes=[vm(dec, total - PRE_COLS), vm(2, query_rows, BLOCK), pltpu.SemaphoreType.DMA, pltpu.SemaphoreType.DMA((2,))],
            compiler_params=pltpu.CompilerParams(vmem_limit_bytes=18 << 20),
            name="project",
        )(x2, pltpu.with_memory_space_constraint(pre, pltpu.VMEM), pltpu.with_memory_space_constraint(dec_out, pltpu.HBM))
        return out[None]

    return jax.shard_map(local_step, mesh=mesh, in_specs=in_specs, out_specs=P("dp", "sp", None), check_vma=False)
```

time: 237 us -> 52.4 us (0.22)
  waiting for transfers between devices: 148 us -> 0 us
  Pallas kernels: 0 us -> 45.4 us
  matrix products: 33.7 us -> 0 us
  blocking collectives: 18.1 us -> 0 us
  between operations: 13.4 us -> 0.17 us
  local copies, waits for them, and re-layouts: 16 us -> 6.43 us
  other arithmetic: 6.93 us -> 0 us
    all_gather x1 -> x0, waiting for transfers between devices: 102 us -> none  [local_step(): return lax.all_gather(out_rows, 'tp', axis=1, tiled=True)]
    pallas_call x0 -> x2, Pallas kernels: none -> 45.4 us  [the longest x1 28.6 us: local_step(): pl.pallas_call(front_kernel, out_shape=(pltpu.VMEM((dec, PRE_COLS), BF16)...]
    dot_general x10 -> x0, matrix products: 32.5 us -> none  [the longest x1 21.1 us: decode_rows(): jnp.dot(final_rows, dec_out, preferred_element_type=jnp.float32)]
    psum x1 -> x0, waiting for transfers between devices: 31.2 us -> none  [local_step(): attn_sum = lax.psum(attn_part, 'tp')]
    all_gather x2 -> x0, blocking collectives: 18.1 us -> none  [the longest x1 9.65 us: local_step(): all_values = lax.all_gather(value_rows, 'tp', axis=1, tiled=True)]
    unnamed x33 -> x0, local copies, waits for them, and re-layouts: 16 us -> none
    reduce_scatter x1 -> x0, waiting for transfers between devices: 15 us -> none  [local_step(): mlp_rows = lax.psum_scatter(mlp_part, 'tp', scatter_dimension=1, tiled=True)]
    reduce_sum x10 -> x0, other arithmetic: 6.44 us -> none  [the longest x4 3.94 us: layer_norm(): row_mean = jnp.mean(widened, axis=-1, keepdims=True)]
  transfers between devices with their start and end apart: 3 -> 0, of which waited for: 3 -> 0; matrix products, arithmetic and copies ran while one was open for 1% -> 0% of each run, Pallas kernels for 0% -> 0%
where the time goes in v1:
time: 52.4 us; the launch traced here: 52 us
  Pallas kernels  45.4 us (87%)
  local copies, waits for them, and re-layouts  6.43 us (12%)
    pallas_call x1, Pallas kernels, local_step(): pl.pallas_call(front_kernel, out_shape=(pltpu.VMEM((dec, PRE_COLS), BF16)...  28.6 us
    pallas_call x1, Pallas kernels, local_step(): pl.pallas_call(out_kernel, out_shape=jax.ShapeDtypeStruct((query_rows, to...  16.7 us
    broadcast_in_dim x1, local copies, waits for them, and re-layouts, local_step(): dec_lnkv[None]  1.3 us
    broadcast_in_dim x1, local copies, waits for them, and re-layouts, local_step(): lat_ln1[None]  1.29 us
    broadcast_in_dim x1, local copies, waits for them, and re-layouts, local_step(): lat_ln2[None]  1.29 us
    broadcast_in_dim x1, local copies, waits for them, and re-layouts, local_step(): dec_lnq[None]  1.28 us
    broadcast_in_dim x1, local copies, waits for them, and re-layouts, local_step(): dec_ln[None]  1.27 us

profile of v1, /device:TPU:0, one launch (start us, length us, event | category | flops | bytes accessed | tf_op | source)
XLA Modules:
  0.0 52.0 jit_solution(2723100960344987021)
XLA Ops:
  0.0 1.3 %broadcast_in_dim.20.gq_in = f32[1,768]{1,0:T(1,128)} reshape(f32[768]{0:T(1024)} %param.30) | data formatting | bytes 6144 | tf_op jit(solution)/shard_map/broadcast_in_dim | solution.py:288
  1.3 1.3 %broadcast_in_dim.22.gd_in = f32[1,768]{1,0:T(1,128)} reshape(f32[768]{0:T(1024)} %param.36) | data formatting | bytes 6144 | tf_op jit(solution)/shard_map/broadcast_in_dim | solution.py:288
  2.6 1.3 %broadcast_in_dim.18.g1_in = f32[1,1280]{1,0:T(1,128)} reshape(f32[1280]{0:T(1024)} %param.22) | data formatting | bytes 10240 | tf_op jit(solution)/shard_map/broadcast_in_dim | solution.py:287
  3.8 1.3 %broadcast_in_dim.19.g2_in = f32[1,1280]{1,0:T(1,128)} reshape(f32[1280]{0:T(1024)} %param.27) | data formatting | bytes 10240 | tf_op jit(solution)/shard_map/broadcast_in_dim | solution.py:288
  5.1 1.3 %broadcast_in_dim.21.gkv_in = f32[1,1280]{1,0:T(1,128)} reshape(f32[1280]{0:T(1024)} %param.31) | data formatting | bytes 10240 | tf_op jit(solution)/shard_map/broadcast_in_dim | solution.py:288
  6.4 28.6 %front.1 = (bf16[768,28160]{1,0:T(8,128)(2,1)S(1)}, bf16[256,768]{1,0:T(8,128)(2,1)}) custom-call(bf16[256,1280]{1,0:T(8,128)(2,1)} %bitcast.13, bf16[256,768]{1,0:T(8,128)(2,1)} %bitcast.14, f32[1,1280]{1,0:T(1,128)} %broadcast_in_dim.18.g1_in, bf16[2,160,1280]{2,1,0:T(8,128)(2,1)} %bitcast.8, bf16[2,160,1280]{2,1,0:T(8,128)(2,1)} %bitcast.9, ...), custom_call_target="tpu_custom_call" | custom-call | tf_op jit(solution)/shard_map/front/pallas_call | solution.py:308
  35.1 16.7 %project.1 = bf16[256,32000]{1,0:T(8,128)(2,1)} custom-call(bf16[256,768]{1,0:T(8,128)(2,1)} %get-tuple-element.7.x_ref, bf16[768,28160]{1,0:T(8,128)(2,1)S(1)} %get-tuple-element.8.pre_ref, bf16[768,32000]{1,0:T(8,128)(2,1)} %rest_hbm.1), custom_call_target="tpu_custom_call" | custom-call | tf_op jit(solution)/shard_map/project/pallas_call | solution.py:317

commit v2 on v1

--- a/solution.py
+++ b/solution.py
@@ -12,9 +12,12 @@
 BF16 = jnp.bfloat16
 F32 = jnp.float32
 
-CHUNKS = 2
-PRE_COLS = 28160
-BLOCK = 6400
+CHUNK_ROWS = (32, 16, 16)
+CHUNKS = len(CHUNK_ROWS)
+PRE_COLS = 26624
+TILE = 256
+TRIP = 4 * TILE
+SLOTS = 6
 
 
 def dot(a, b):
@@ -46,7 +49,7 @@
 def front_kernel(
     lat_in, qry_in, g1_in, wq_in, wk_in, wv_in, wo_in, g2_in, up_in, down_in,
     gq_in, gkv_in, dwq_in, dwk_in, dwv_in, dwo_in, gd_in, dup_in, ddown_in, out_in,
-    pre_out, x2_out,
+    pre_out,
     z, normed, qry, g1, g2, gq, gkv, gd, wq, wk, wv, wo, up, down, dwq, dwk, dwv, dwo, dup, ddown,
     q_h, k_h, v_h, ctx_mine, ctx_send, ctx_recv,
     part1, recv1, mid, part2, recv2, kv_in, qd, kd, vd, mixed,
@@ -63,7 +66,7 @@
     rows = z.shape[0]
     half = rows // 2
     mine = half // 2
-    step = mine // CHUNKS
+    starts = [sum(CHUNK_ROWS[:k]) for k in range(CHUNKS)]
     mlp = down_in.shape[0]
 
     barrier = pltpu.get_barrier_semaphore()
@@ -102,7 +105,7 @@
     pre = []
     for i in range(pre_pieces):
         band = pl.ds(i * pre_rows, pre_rows)
-        copy = pltpu.make_async_copy(out_in.at[band, pl.ds(0, PRE_COLS)], pre_out.at[band], pre_sem.at[i])
+        copy = pltpu.make_async_copy(out_in.at[band, pl.ds(0, PRE_COLS)], pre_out.at[band, pl.ds(0, PRE_COLS)], pre_sem.at[i])
         copy.start(priority=1)
         pre.append(copy)
 
@@ -113,16 +116,13 @@
         copy.start()
         return copy
 
+    loads["z"].wait()
+    loads["g1"].wait()
+    gain1 = g1[...][None, :]
+    for r in range(0, rows, 16):
+        normed[pl.ds(r, 16), :] = norm_rows(z[pl.ds(r, 16), :].astype(F32), gain1)
     pl.semaphore_wait(barrier, 3)
     swap_wo = send(0, wo_in, wo.at[pl.ds(heads * head_dim, heads * head_dim)], partner)
-    swap_up = send(1, up_in, up.at[pl.ds(mlp, mlp)], partner)
-    swap_down = send(2, down_in, down.at[pl.ds(mlp, mlp)], partner)
-
-    loads["z"].wait()
-    loads["g1"].wait()
-    gain1 = g1[...]
-    for r in range(0, rows, 16):
-        normed[pl.ds(r, 16), :] = norm_rows(z[pl.ds(r, 16), :].astype(F32), gain1)
     loads["wk"].wait()
     for h in range(heads):
         k_h[h] = dot_nt(normed[...], wk[h]).astype(BF16)
@@ -142,6 +142,8 @@
 
     attend(pl.multiple_of((1 - c) * mine, mine), ctx_send)
     swap_ctx = send(3, ctx_send, ctx_recv, partner)
+    swap_up = send(1, up_in, up.at[pl.ds(mlp, mlp)], partner)
+    swap_down = send(2, down_in, down.at[pl.ds(mlp, mlp)], partner)
     attend(pl.multiple_of(c * mine, mine), ctx_mine)
 
     loads["wo"].wait()
@@ -150,7 +152,7 @@
     first_sends, second_sends, kv_part, kv_y, kv_fwd = [], [], [], [], []
     base = 4
     for k in range(CHUNKS):
-        band = pl.ds(k * step, step)
+        band = pl.ds(starts[k], CHUNK_ROWS[k])
         total = None
         for src, row0 in ((ctx_mine, 0), (ctx_recv, heads * head_dim)):
             for h in range(heads):
@@ -162,7 +164,7 @@
     loads["qry"].wait()
     loads["gq"].wait()
     loads["dwq"].wait()
-    gain_q = gq[...]
+    gain_q = gq[...][None, :]
     query_rows = qry.shape[0]
     for r in range(0, query_rows, 16):
         mixed[pl.ds(r, 16), :] = norm_rows(qry[pl.ds(r, 16), :].astype(F32), gain_q)
@@ -172,14 +174,14 @@
         loads[name].wait()
     swap_up.wait()
     swap_down.wait()
-    gain2 = g2[...]
-    gain_kv = gkv[...]
+    gain2 = g2[...][None, :]
+    gain_kv = gkv[...][None, :]
     base = 4 + CHUNKS
     row_first = s * half + c * mine
     for k in range(CHUNKS):
-        band = pl.ds(k * step, step)
+        band = pl.ds(starts[k], CHUNK_ROWS[k])
         first_sends[k].wait()
-        zrows = z[pl.ds(pl.multiple_of(row_first + k * step, step), step), :].astype(F32)
+        zrows = z[pl.ds(pl.multiple_of(row_first + starts[k], 16), CHUNK_ROWS[k]), :].astype(F32)
         mid[band, :] = (zrows + (part1[band, :].astype(F32) + recv1[band, :].astype(F32))).astype(BF16)
         hidden = gelu(dot_nt(norm_rows(mid[band, :].astype(F32), gain2), up[...])).astype(BF16)
         part2[band, :] = dot(hidden, down[...]).astype(BF16)
@@ -187,7 +189,7 @@
 
     base = 4 + 2 * CHUNKS
     for k in range(CHUNKS):
-        band = pl.ds(k * step, step)
+        band = pl.ds(starts[k], CHUNK_ROWS[k])
         second_sends[k].wait()
         full = mid[band, :].astype(F32) + (part2[band, :].astype(F32) + recv2[band, :].astype(F32))
         kv_in[0, band, :] = norm_rows(full.astype(BF16).astype(F32), gain_kv)
@@ -208,7 +210,7 @@
     keys_values(0)
     base = 4 + 4 * CHUNKS
     for k in range(CHUNKS):
-        band = pl.ds(k * step, step)
+        band = pl.ds(starts[k], CHUNK_ROWS[k])
         kv_y[k].wait()
         kv_fwd.append(send(base + k, kv_in.at[2, band], kv_in.at[3, band], partner))
     for k in range(CHUNKS):
@@ -217,7 +219,7 @@
 
     for name in ("dwo", "gd", "dup", "ddown"):
         loads[name].wait()
-    gain_d = gd[...]
+    gain_d = gd[...][None, :]
     blk = query_rows // 2
     for q in range(2):
         band = pl.ds(q * blk, blk)
@@ -227,42 +229,123 @@
     for q in range(2):
         band = pl.ds(q * blk, blk)
         hidden = gelu(dot(norm_rows(mixed[band, :].astype(F32), gain_d), dup[...])).astype(BF16)
-        x2_out[band, :] = (mixed[band, :].astype(F32) + dot(hidden, ddown[...])).astype(BF16)
+        pre_out[band, pl.ds(PRE_COLS, qd.shape[1])] = (mixed[band, :].astype(F32) + dot(hidden, ddown[...])).astype(BF16)
 
     for copy in pre:
         copy.wait()
 
 
-def out_kernel(x_ref, pre_ref, rest_hbm, o_ref, rest, stage, rest_sem, out_sem):
-    total = o_ref.shape[1]
-    pre_cols = pre_ref.shape[1]
-    fetch = pltpu.make_async_copy(rest_hbm.at[:, pl.ds(pre_cols, total - pre_cols)], rest, rest_sem)
+def out_kernel(pre_ref, rest_hbm, o_ref, rest, stage, rest_sem, out_sem):
+    rows = o_ref.shape[0]
+    depth = pre_ref.shape[0]
+    passes = depth // TILE
+    x_col = PRE_COLS
+    fetch = pltpu.make_async_copy(rest_hbm.at[:, pl.ds(PRE_COLS, rest.shape[1])], rest, rest_sem)
     fetch.start()
-    copies = []
-    first = 0
-    widths = []
-    left = pre_cols
-    while left:
-        widths.append((min(BLOCK, left), False))
-        left -= widths[-1][0]
-    left = total - pre_cols
-    while left:
-        widths.append((min(2560, left), True))
-        left -= widths[-1][0]
-    for i, (width, from_rest) in enumerate(widths):
-        slot = i % 2
-        if i >= 2:
-            copies[i - 2].wait()
-        if from_rest and not widths[i - 1][1]:
-            fetch.wait()
-        src, off = (rest, first - pre_cols) if from_rest else (pre_ref, first)
-        stage[slot, :, pl.ds(0, width)] = dot(x_ref[...], src[:, pl.ds(off, width)]).astype(BF16)
-        copy = pltpu.make_async_copy(stage.at[slot, :, pl.ds(0, width)], o_ref.at[:, pl.ds(first, width)], out_sem.at[slot])
-        copy.start()
-        copies.append(copy)
-        first += width
-    copies[-2].wait()
-    copies[-1].wait()
+    trips = o_ref.shape[1] // TRIP
+    pre_trips = PRE_COLS // TRIP
+    slots = stage.shape[0]
+
+    def lhs(k, row0=0, count=rows):
+        return pre_ref[pl.ds(row0, count), pl.ds(x_col + k * TILE, TILE)]
+
+    def body(accs, small):
+        def push(src, col, k, reg, apart=TILE):
+            for q in range(2):
+                cols = pl.ds(pl.multiple_of(col + q * apart, TILE), TILE)
+                pltpu.matmul_push_rhs(src[pl.ds(k * TILE, TILE), cols], staging_register=reg, mxu_index=q)
+
+        def out_copy(trip, slot):
+            cols = pl.ds(pl.multiple_of(trip * TRIP - TRIP // 2, TRIP // 2), TRIP)
+            return pltpu.make_async_copy(stage.at[slot], o_ref.at[:, cols], out_sem.at[slot])
+
+        def pop(acc_pair, slot, part):
+            for q in range(2):
+                stage[slot, :, pl.ds((2 * part + q) * TILE, TILE)] = pltpu.matmul_pop(acc_pair[q]).astype(BF16)
+
+        def one_trip(src, col, slot, next_src, next_col, apart=TILE):
+            reg = 0
+            for pair in range(2):
+                for k in range(passes):
+                    for q in range(2):
+                        pltpu.matmul_acc_lhs(accs[pair][q], lhs(k), load_staged_rhs=reg)
+                    reg = 1 - reg
+                    if k + 1 < passes:
+                        push(src, col + pair * 2 * TILE, k + 1, reg)
+                    elif pair == 0:
+                        push(src, col + 2 * TILE, 0, reg)
+                    else:
+                        push(next_src, next_col, 0, reg, apart)
+                    if k == 0:
+                        pop(accs[1 - pair], slot, pair)
+
+        def trip_at(i, src, col, next_src, next_col, wait, apart=TILE):
+            slot = lax.rem(i, slots)
+            if wait:
+                out_copy(i - slots, slot).wait()
+            one_trip(src, col, slot, next_src, next_col, apart)
+            out_copy(i, slot).start()
+
+        for pair in accs:
+            for acc in pair:
+                pltpu.matmul_pop(acc)
+        for acc in small:
+            pltpu.matmul_pop(acc)
+
+        push(pre_ref, 0, 0, 0)
+        one_trip(pre_ref, 0, 0, pre_ref, TRIP)
+        head = pltpu.make_async_copy(stage.at[0, :, pl.ds(TRIP // 2, TRIP // 2)], o_ref.at[:, pl.ds(0, TRIP // 2)], out_sem.at[0])
+        head.start()
+
+        def early(i, carry):
+            trip_at(i, pre_ref, i * TRIP, pre_ref, (i + 1) * TRIP, False)
+            return carry
+
+        def late(i, carry):
+            trip_at(i, pre_ref, i * TRIP, pre_ref, (i + 1) * TRIP, True)
+            return carry
+
+        def tail(i, carry):
+            col = (i - pre_trips) * TRIP
+            trip_at(i, rest, col, rest, col + TRIP, True)
+            return carry
+
+        lax.fori_loop(1, slots, early, 0)
+        head.wait()
+        trip_at(slots, pre_ref, slots * TRIP, pre_ref, (slots + 1) * TRIP, False)
+        lax.fori_loop(slots + 1, pre_trips - 1, late, 0)
+        fetch.wait()
+        last = pre_trips - 1
+        trip_at(last, pre_ref, last * TRIP, rest, 0, True)
+        lax.fori_loop(pre_trips, trips - 1, tail, 0)
+
+        slot = trips % slots
+        col = trips * TRIP - PRE_COLS
+        trip_at(trips - 1, rest, col - TRIP, rest, col, True, 0)
+        half = rows // 2
+        out_copy(trips - slots, slot).wait()
+        reg = 0
+        for k in range(passes):
+            for q in range(2):
+                pltpu.matmul_acc_lhs(small[q], lhs(k, q * half, half), load_staged_rhs=reg)
+            reg = 1 - reg
+            if k + 1 < passes:
+                push(rest, col, k + 1, reg, 0)
+            if k == 0:
+                pop(accs[1], slot, 0)
+                near = pltpu.make_async_copy(stage.at[slot, :, pl.ds(0, TRIP // 2)], o_ref.at[:, pl.ds(trips * TRIP - TRIP // 2, TRIP // 2)], out_sem.at[slot])
+                near.start()
+        for q in range(2):
+            stage[slot, pl.ds(q * half, half), pl.ds(TRIP // 2, TILE)] = pltpu.matmul_pop(small[q]).astype(BF16)
+        end = pltpu.make_async_copy(stage.at[slot, :, pl.ds(TRIP // 2, TILE)], o_ref.at[:, pl.ds(trips * TRIP, TILE)], out_sem.at[slots])
+        end.start()
+        for i in range(trips - slots + 1, trips):
+            out_copy(i, i % slots).wait()
+        near.wait()
+        end.wait()
+
+    acc = [[pltpu.ACC(q)((rows, TILE), F32) for q in range(2)] for _ in range(2)]
+    pl.run_scoped(body, acc, [pltpu.ACC(q)((rows // 2, TILE), F32) for q in range(2)])
 
 
 def solution(mesh):
@@ -284,8 +367,8 @@
             return jnp.transpose(w, (1, 2, 0))
 
         args = [
-            latents[0], queries[0], lat_ln1[None], flip(lat_wq), flip(lat_wk), flip(lat_wv), lat_wo.reshape(heads * head_dim, width),
-            lat_ln2[None], lat_up.T, lat_down, dec_lnq[None], dec_lnkv[None], dec_wq, dec_wk, dec_wv, dec_wo, dec_ln[None], dec_up, dec_down, dec_out,
+            latents[0], queries[0], lat_ln1, flip(lat_wq), flip(lat_wk), flip(lat_wv), lat_wo.reshape(heads * head_dim, width),
+            lat_ln2, lat_up.T, lat_down, dec_lnq, dec_lnkv, dec_wq, dec_wk, dec_wv, dec_wo, dec_ln, dec_up, dec_down, dec_out,
         ]
         args = [pltpu.with_memory_space_constraint(a, pltpu.HBM) for a in args]
 
@@ -294,7 +377,7 @@
 
         scratch = [
             vm(rows, width), vm(rows, width), vm(query_rows, query_ch),
-            vm(1, width, dtype=F32), vm(1, width, dtype=F32), vm(1, query_ch, dtype=F32), vm(1, width, dtype=F32), vm(1, dec, dtype=F32),
+            vm(width, dtype=F32), vm(width, dtype=F32), vm(query_ch, dtype=F32), vm(width, dtype=F32), vm(dec, dtype=F32),
             vm(heads, head_dim, width), vm(heads, head_dim, width), vm(heads, head_dim, width),
             vm(2 * heads * head_dim, width), vm(2 * mlp, width), vm(2 * mlp, width),
             vm(query_ch, dec), vm(width, dec), vm(width, dec), vm(dec, dec), vm(dec, dec), vm(dec, dec),
@@ -305,11 +388,11 @@
             pltpu.SemaphoreType.DMA((19,)), pltpu.SemaphoreType.DMA((8,)),
             pltpu.SemaphoreType.DMA((4 + 5 * CHUNKS,)), pltpu.SemaphoreType.DMA((4 + 5 * CHUNKS,)),
         ]
-        pre, x2 = pl.pallas_call(
+        pre = pl.pallas_call(
             front_kernel,
-            out_shape=(pltpu.VMEM((dec, PRE_COLS), BF16), jax.ShapeDtypeStruct((query_rows, dec), BF16)),
+            out_shape=pltpu.VMEM((dec, PRE_COLS + dec), BF16),
             in_specs=[pl.BlockSpec(memory_space=pltpu.HBM)] * len(args),
-            out_specs=(pl.BlockSpec(memory_space=pltpu.VMEM), pl.BlockSpec(memory_space=pltpu.VMEM)),
+            out_specs=pl.BlockSpec(memory_space=pltpu.VMEM),
             scratch_shapes=scratch,
             compiler_params=pltpu.CompilerParams(collective_id=0, has_side_effects=True, vmem_limit_bytes=22 << 20),
             name="front",
@@ -317,12 +400,12 @@
         out = pl.pallas_call(
             out_kernel,
             out_shape=jax.ShapeDtypeStruct((query_rows, total), BF16),
-            in_specs=[pl.BlockSpec(memory_space=pltpu.VMEM), pl.BlockSpec(memory_space=pltpu.VMEM), pl.BlockSpec(memory_space=pltpu.HBM)],
+            in_specs=[pl.BlockSpec(memory_space=pltpu.VMEM), pl.BlockSpec(memory_space=pltpu.HBM)],
             out_specs=pl.BlockSpec(memory_space=pltpu.HBM),
-            scratch_shapes=[vm(dec, total - PRE_COLS), vm(2, query_rows, BLOCK), pltpu.SemaphoreType.DMA, pltpu.SemaphoreType.DMA((2,))],
+            scratch_shapes=[vm(dec, total - PRE_COLS), vm(SLOTS, query_rows, TRIP), pltpu.SemaphoreType.DMA, pltpu.SemaphoreType.DMA((SLOTS + 1,))],
             compiler_params=pltpu.CompilerParams(vmem_limit_bytes=18 << 20),
             name="project",
-        )(x2, pltpu.with_memory_space_constraint(pre, pltpu.VMEM), pltpu.with_memory_space_constraint(dec_out, pltpu.HBM))
+        )(pltpu.with_memory_space_constraint(pre, pltpu.VMEM), pltpu.with_memory_space_constraint(dec_out, pltpu.HBM))
         return out[None]
 
     return jax.shard_map(local_step, mesh=mesh, in_specs=in_specs, out_specs=P("dp", "sp", None), check_vma=False)

time: 52.4 us -> 40.1 us (0.77)
  local copies, waits for them, and re-layouts: 6.43 us -> 0 us
  Pallas kernels: 45.4 us -> 40 us
    broadcast_in_dim x5 -> x0, local copies, waits for them, and re-layouts: 6.43 us -> none  [the longest x1 1.3 us: local_step(): dec_lnkv[None]]
    pallas_call x1, Pallas kernels: 28.6 us -> 25.7 us  [local_step(): pl.pallas_call(front_kernel, out_shape=pltpu.VMEM((dec, PRE_COLS + dec),...]
    pallas_call x1, Pallas kernels: 16.7 us -> 14.3 us  [local_step(): pl.pallas_call(out_kernel, out_shape=jax.ShapeDtypeStruct((query_rows, to...]
where the time goes in v2:
time: 40.1 us; the launch traced here: 40 us
  Pallas kernels  40 us (100%)
    pallas_call x1, Pallas kernels, local_step(): pl.pallas_call(front_kernel, out_shape=pltpu.VMEM((dec, PRE_COLS + dec),...  25.7 us
    pallas_call x1, Pallas kernels, local_step(): pl.pallas_call(out_kernel, out_shape=jax.ShapeDtypeStruct((query_rows, to...  14.3 us

profile of v2, /device:TPU:0, one launch (start us, length us, event | category | flops | bytes accessed | tf_op | source)
XLA Modules:
  0.0 40.0 jit_solution(9027332497176955254)
XLA Ops:
  0.0 25.7 %front.1.pre_ref = bf16[768,27392]{1,0:T(8,128)(2,1)S(1)} custom-call(bf16[256,1280]{1,0:T(8,128)(2,1)} %bitcast.13, bf16[256,768]{1,0:T(8,128)(2,1)} %bitcast.14, f32[1280]{0:T(1024)} %g1_in.1, bf16[2,160,1280]{2,1,0:T(8,128)(2,1)} %bitcast.8, bf16[2,160,1280]{2,1,0:T(8,128)(2,1)} %bitcast.9, bf16[2,160,1280]{2,1,0:T(8,128)(2,1)} %bitcast.10, ...), custom_call_target="tpu_custom_call" | custom-call | tf_op jit(solution)/shard_map/front/pallas_call | solution.py:391
  25.7 14.3 %project.1 = bf16[256,32000]{1,0:T(8,128)(2,1)} custom-call(bf16[768,27392]{1,0:T(8,128)(2,1)S(1)} %front.1.pre_ref, bf16[768,32000]{1,0:T(8,128)(2,1)} %rest_hbm.1), custom_call_target="tpu_custom_call" | custom-call | tf_op jit(solution)/shard_map/project/pallas_call | solution.py:400
